TPU v7x, 128 devices: a whole 4x4x4 slice. The times are simulated.
128 devices in a mesh: row: 8 (over z, y_lo), col: 16 (over y_hi, x, core).
Axes of the slice: x: 4, y: 4 (y_hi: 2, y_lo: 2; y = y_hi * 2 + y_lo), z: 4, core: 2. Of those that a mesh axis runs over, the one named last changes fastest.
Arguments:
- joined_weight: bfloat16 [16, 2880, 5760], P('row', 'col'), may hold values from -0.109375 to 0.109375
- tile_perm: int32 [144], replicated, may hold values from 0 to 143, each once
- down_weight: bfloat16 [16, 2880, 2880], P('row', 'col'), may hold values from -0.109375 to 0.109375
- tokens: bfloat16 [1024, 2880], P(('row', 'col')), may hold values from -6 to 6
- expert_ids: int32 [1024, 4], replicated, may hold values from 0 to 15, all different within a row; in each aligned block of 1024 rows (0 to 1023, 1024 to 2047, ...) at most 512 rows name the same one
- route_scores: float32 [1024, 4], replicated, may hold values from 0.1 to 1
Outputs:
- gate_weight: bfloat16 [16, 2880, 2880], P('row', None, 'col')
- up_weight: bfloat16 [16, 2880, 2880], P('row', None, 'col')
- mixed: bfloat16 [1024, 2880], P(('row', 'col'))
Inputs may be any that keep to these rules, and one draw needn't show every extreme that they name: `expert_ids`: every expert is chosen by at most 512 tokens, a bound that some block reaches.
All inputs are finite; a program needn't handle non-finite values.
Results may differ from a plain program's by a relative error of at most 0.0049.
Values may be sent and summed in bfloat16 or wider, within the bound.
No kernel may reach another device: no remote copies, remote signals or barrier semaphores. Data moves between devices by JAX's collectives and lax.ppermute only.
A program may use at most 128 MiB of HBM per device.

v0:
```python
import jax
import jax.numpy as jnp
from jax import lax
from jax.sharding import PartitionSpec as P


def body(joined_weight, tile_perm, down_weight, tokens, expert_ids, route_scores):
    n_col = lax.axis_size("col")
    local = joined_weight.shape[0]
    width = joined_weight.shape[2]
    ff_local = width // 2 // n_col
    tiles = tile_perm.shape[0]
    tile_cols = width // tiles
    places = jnp.arange(tiles, dtype=jnp.int32)
    inverse = jnp.sum(places[:, None] * (tile_perm[:, None] == places[None, :]), axis=0)
    order = jnp.arange(width, dtype=jnp.int32)
    lookup = (order // tile_cols)[:, None] == places[None, :]
    stored = jnp.sum(lookup * inverse[None, :], axis=1) * tile_cols + order % tile_cols
    packed = jnp.take(joined_weight, stored, axis=2)
    everything = lax.all_gather(tokens, ("row", "col"), axis=0, tiled=True)
    expert_global = lax.axis_index("row") * local + jnp.arange(local, dtype=jnp.int32)
    weights = route_scores / jnp.sum(route_scores, axis=1, keepdims=True)
    share = jnp.sum(
        weights[:, :, None] * (expert_ids[:, :, None] == expert_global[None, None, :]), axis=1
    )
    weights_in = lax.all_to_all(packed, "col", split_axis=2, concat_axis=1, tiled=True)
    count = weights_in.shape[0]
    paired = weights_in.reshape(count, weights_in.shape[1], ff_local, 2)
    gate_part = paired[:, :, :, 0]
    up_part = paired[:, :, :, 1]
    pre_gate = jnp.einsum("td,ndf->ntf", everything, gate_part, preferred_element_type=jnp.float32)
    pre_up = jnp.einsum("td,ndf->ntf", everything, up_part, preferred_element_type=jnp.float32)
    gate_out, up_out = (gate_part, up_part)
    pre_gate, pre_up = (pre_gate, pre_up)
    active = share.T[:, :, None] * (pre_up + 1.0) * pre_gate * jax.nn.sigmoid(1.702 * pre_gate)
    active = active.astype(jnp.bfloat16)
    total = lax.psum_scatter(
        jnp.einsum("ntf,nfd->td", active, down_weight, preferred_element_type=jnp.float32),
        ("row", "col"),
        scatter_dimension=0,
        tiled=True,
    )
    return (gate_out, up_out, total.astype(jnp.bfloat16))


def solution(mesh):
    placed = (P("row", "col", None), P(), P("row", "col", None), P(("row", "col"), None), P(), P())
    return jax.shard_map(
        body,
        mesh=mesh,
        in_specs=placed,
        out_specs=(P("row", None, "col"), P("row", None, "col"), P(("row", "col"), None)),
        check_vma=False,
    )
```

profile of v0, /device:TPU:0, one launch (start us, length us, event | category | flops | bytes accessed | tf_op | source)
XLA Modules:
  0.0 425.9 jit_solution(15690301397363890240)
XLA Ops:
  7.2 0.0 copy-start
  7.2 0.0 all-gather.2.cloned.1.call-start
  7.2 0.7 all-gather.2.cloned.1.call-update
  7.9 0.0 copy-start.5
  7.9 19.8 %copy.38 = bf16[2,180,5760]{1,0,2:T(2,128)(2,1)} copy(bf16[2,180,5760]{2,0,1:T(2,128)(2,1)} %param.6) | data formatting | bytes 8294400 | tf_op args[0]
  27.7 0.0 copy-done.5
  27.7 0.1 select_reduce_fusion.1
  27.8 0.6 select_reduce_fusion
  28.4 0.1 fusion.22
  28.6 25.1 %gather_fusion = bf16[5760,2,180]{2,1,0:T(2,128)(2,1)} fusion(bf16[2,180,5760]{1,0,2:T(2,128)(2,1)} %copy.38, s32[6144]{0:T(1024)S(1)} %pad_clamp_fusion), kind=kCustom, calls=%fused_computation | custom fusion | bytes 8317440 | tf_op jit(solution)/shard_map/jit(_take)/gather | solution.py:19
  53.7 22.9 %fusion.4 = bf16[2,180,5760]{1,0,2:T(2,128)(2,1)} fusion(bf16[5760,2,180]{2,1,0:T(2,128)(2,1)} %gather_fusion, pred[5760]{0:T(1024)(128)(4,1)S(1)} %compare_and_fusion), kind=kLoop, calls=%fused_computation.8 | loop fusion | flops 2073600 | bytes 8300160 | tf_op jit(solution)/shard_map/jit(_take)/select_n | solution.py:19
  76.6 7.4 %all-to-all-start = ((bf16[2,180,5760]{1,0,2:T(2,128)(2,1)}), bf16[2,180,5760]{1,0,2:T(2,128)(2,1)}, u32[]{:S(2)}, u32[]{:S(2)}) async-start(bf16[2,180,5760]{1,0,2:T(2,128)(2,1)} %fusion.4), calls=%async_computation | async-start | bytes 11796480 | tf_op jit(solution)/shard_map/all_to_all | solution.py:26
  84.0 0.0 copy-done.3
  84.1 0.0 copy-done.4
  84.1 0.1 select_reduce_fusion.2
  84.2 80.8 %all-to-all-done = bf16[2,180,5760]{1,0,2:T(2,128)(2,1)} async-done(((bf16[2,180,5760]{1,0,2:T(2,128)(2,1)}), bf16[2,180,5760]{1,0,2:T(2,128)(2,1)}, u32[]{:S(2)}, u32[]{:S(2)}) %all-to-all-start) | async-done | bytes 4147232 | tf_op jit(solution)/shard_map/all_to_all | solution.py:26
  165.0 7.3 %copy.51 = bf16[2,180,16,360]{1,2,3,0:T(8,128)(2,1)} copy(bf16[2,180,16,360]{1,0,3,2:T(2,128)(2,1)} %bitcast.1) | data formatting | bytes 8294400 | tf_op jit(solution)/shard_map/all_to_all | solution.py:26
  172.3 18.4 %reshape.79 = bf16[2,2880,180,2]{1,3,2,0:T(2,128)(2,1)} reshape(bf16[2,16,180,360]{2,1,3,0:T(8,128)(2,1)} %bitcast.36) | data formatting | bytes 8294400 | tf_op jit(solution)/shard_map/reshape | solution.py:28
  190.7 9.2 %fusion.25 = (bf16[2,2880,180,1]{1,3,2,0:T(2,128)(2,1)S(1)}, bf16[2,2880,180,1]{1,3,2,0:T(2,128)(2,1)S(1)}) fusion(bf16[2,2880,180,2]{1,3,2,0:T(2,128)(2,1)} %reshape.79), kind=kLoop, calls=%fused_computation.44 | loop fusion | bytes 8294400 | tf_op jit(solution)/shard_map/slice | solution.py:30
  199.9 0.2 copy.52
  200.2 0.0 copy-start.1
  200.2 3.0 copy.42
  203.1 0.2 copy.53
  203.4 0.0 copy-done.1
  203.4 0.0 copy-start.2
  203.4 1.3 copy-done.2
  204.7 3.0 copy.43
  207.7 69.3 %all-gather.2.cloned.1.call-done = bf16[1024,2880]{1,0:T(8,128)(2,1)} async-done(((bf16[8,2880]{1,0:T(8,128)(2,1)}), bf16[1024,2880]{1,0:T(8,128)(2,1)}) %all-gather.2.cloned.1.call-update) | async-done | bytes 5898256 | tf_op jit(solution)/shard_map/all_gather | solution.py:20
  277.0 7.1 %fusion = f32[2,180,1024]{2,1,0:T(8,128)} fusion(bf16[2,2880,180]{1,2,0:T(8,128)(2,1)} %bitcast.38, bf16[1024,2880]{1,0:T(8,128)(2,1)} %all-gather.2.cloned.1.call-done), kind=kOutput, calls=%fused_computation.3 | convolution fusion | flops 2123366400 | bytes 9446400 | tf_op jit(solution)/shard_map/td,ndf->ntf/dot_general | solution.py:31
  284.0 14.3 %convolution_bitcast_fusion = f32[1024,2880]{1,0:T(8,128)} fusion(bf16[2,180,2880]{2,0,1:T(2,128)(2,1)S(1)} %copy-done, f32[2,180,1024]{2,1,0:T(8,128)} %fusion, bf16[2,2880,180]{1,2,0:T(8,128)(2,1)} %bitcast.40, bf16[1024,2880]{1,0:T(8,128)(2,1)} %all-gather.2.cloned.1.call-done, f32[2,1024]{1,0:T(2,128)S(1)} %bitcast.41), kind=kOutput, calls=%fused_computation.2 | convolution fusion | flops 4250050560 | bytes 23324672 | tf_op jit(solution)/shard_map/ntf,nfd->td/dot_general | solution.py:38
  298.4 119.3 %all-reduce.2 = bf16[1024,2880]{1,0:T(8,128)(2,1)} all-reduce(f32[1024,2880]{1,0:T(8,128)} %convolution_bitcast_fusion), channel_id=2, replica_groups=mesh['row'=8,'col'=16] {'row','col'}, use_global_device_ids=true, to_apply=%region_4.5.clone | all-reduce | flops 2949120 | bytes 17694720
  417.6 1.4 dynamic-slice_convert_fusion
  (10 shorter events, 0.1 us)
Async XLA Ops:
  7.2 276.9 %copy-start = (bf16[2,180,2880]{2,0,1:T(2,128)(2,1)S(1)}, bf16[2,180,2880]{2,0,1:T(2,128)(2,1)}, u32[]{:S(2)}) copy-start(bf16[2,180,2880]{2,0,1:T(2,128)(2,1)} %param.8) | copy-start | bytes 6220804
  7.2 269.8 %all-gather.2.cloned.1.call-start = ((), (), s32[]{:S(2)}) async-start(), calls=%async_computation.1 | async-start | bytes 6076416 | tf_op jit(solution)/shard_map/all_gather | solution.py:20
  7.9 19.8 %copy-start.5 = (s32[144]{0:T(256)S(1)}, s32[144]{0:T(256)}, u32[]{:S(2)}) copy-start(s32[144]{0:T(256)} %param.7) | copy-start | bytes 1732
  76.6 7.4 %copy-start.3 = (f32[1024,4]{0,1:T(4,128)S(1)}, f32[1024,4]{0,1:T(4,128)}, u32[]{:S(2)}) copy-start(f32[1024,4]{0,1:T(4,128)} %param.11) | copy-start | bytes 49156
  76.6 7.5 %copy-start.4 = (s32[1024,4]{0,1:T(4,128)S(1)}, s32[1024,4]{0,1:T(4,128)}, u32[]{:S(2)}) copy-start(s32[1024,4]{0,1:T(4,128)} %param.10) | copy-start | bytes 49156
  76.6 88.3 %all-to-all-start = ((bf16[2,180,5760]{1,0,2:T(2,128)(2,1)}), bf16[2,180,5760]{1,0,2:T(2,128)(2,1)}, u32[]{:S(2)}, u32[]{:S(2)}) async-start(bf16[2,180,5760]{1,0,2:T(2,128)(2,1)} %fusion.4), calls=%async_computation | async-start | bytes 11796480 | tf_op jit(solution)/shard_map/all_to_all | solution.py:26
  200.2 3.2 copy-start.1
  203.4 1.3 copy-start.2
Sparse Core Ops, SparseCore 0:
  9.7 267.2 all-gather.1
where the time goes:
time: 427 us; the launch traced here: 426 us
  waiting for transfers between devices  151 us (35%)
  blocking collectives  119 us (28%)
  local copies, waits for them, and re-layouts  89 us (21%)
  other arithmetic  23.9 us (6%)
  matrix products  21.4 us (5%)
  between operations  14.2 us (3%)
  starting transfers between devices  7.42 us (2%)
    unnamed x1, blocking collectives  119 us
    all_to_all x1, waiting for transfers between devices, body(): lax.all_to_all(packed, 'col', split_axis=2, concat_axis=1, tiled=True)  80.8 us
    all_gather x1, waiting for transfers between devices, body(): everything = lax.all_gather(tokens, ('row', 'col'), axis=0, tiled=True)  69.3 us
    unnamed x17, local copies, waits for them, and re-layouts  27.5 us
    gather x1, local copies, waits for them, and re-layouts, body(): packed = jnp.take(joined_weight, stored, axis=2)  25.1 us
    select_n x2, other arithmetic, body(): packed = jnp.take(joined_weight, stored, axis=2)  23.1 us
    reshape x1, local copies, waits for them, and re-layouts, body(): paired = weights_in.reshape(count, weights_in.shape[1], ff_local, 2)  18.4 us
    dot_general x1, matrix products, body(): jnp.einsum('ntf,nfd->td', active, down_weight, preferred_element_type=jnp...  14.3 us
  transfers between devices with their start and end apart: 2, of which 2 were waited for; matrix products, arithmetic and copies ran while one was open for 26% of the time, Pallas kernels for 0%

commit v1 on v0

--- a/solution.py
+++ b/solution.py
@@ -17,7 +17,12 @@
     lookup = (order // tile_cols)[:, None] == places[None, :]
     stored = jnp.sum(lookup * inverse[None, :], axis=1) * tile_cols + order % tile_cols
     packed = jnp.take(joined_weight, stored, axis=2)
-    everything = lax.all_gather(tokens, ("row", "col"), axis=0, tiled=True)
+    all_rows = []
+    for _ in range(lax.axis_size(("row", "col"))):
+        all_rows.append(tokens)
+    everything = jnp.concatenate(
+        lax.all_to_all(jnp.stack(all_rows, axis=0), ("row", "col"), 0, 0), axis=0
+    )
     expert_global = lax.axis_index("row") * local + jnp.arange(local, dtype=jnp.int32)
     weights = route_scores / jnp.sum(route_scores, axis=1, keepdims=True)
     share = jnp.sum(

time: 427 us -> 372 us (0.87)
  waiting for transfers between devices: 151 us -> 29 us
  blocking collectives: 119 us -> 196 us
  between operations: 14.2 us -> 0.82 us
    all_to_all x0 -> x1, blocking collectives: none -> 76.8 us  [body(): lax.all_to_all(packed, 'col', split_axis=2, concat_axis=1, tiled=True)]
    all_gather x1 -> x0, waiting for transfers between devices: 69.3 us -> none  [body(): everything = lax.all_gather(tokens, ('row', 'col'), axis=0, tiled=True)]
    all_to_all x1, waiting for transfers between devices: 80.8 us -> 29 us  [body(): lax.all_to_all(jnp.stack(all_rows, axis=0), ('row', 'col'), 0, 0)]
  transfers between devices with their start and end apart: 2 -> 1, of which waited for: 2 -> 1; matrix products, arithmetic and copies ran while one was open for 26% -> 11% of each run, Pallas kernels for 0% -> 0%
where the time goes in v1:
time: 372 us; the launch traced here: 370 us
  blocking collectives  196 us (53%)
  local copies, waits for them, and re-layouts  92.1 us (25%)
  waiting for transfers between devices  29 us (8%)
  other arithmetic  24.2 us (7%)
  matrix products  21.1 us (6%)
  starting transfers between devices  7.45 us (2%)
    unnamed x1, blocking collectives  119 us
    all_to_all x1, blocking collectives, body(): lax.all_to_all(packed, 'col', split_axis=2, concat_axis=1, tiled=True)  76.8 us
    all_to_all x1, waiting for transfers between devices, body(): lax.all_to_all(jnp.stack(all_rows, axis=0), ('row', 'col'), 0, 0)  29 us
    unnamed x17, local copies, waits for them, and re-layouts  27.5 us
    gather x1, local copies, waits for them, and re-layouts, body(): packed = jnp.take(joined_weight, stored, axis=2)  25.1 us
    select_n x2, other arithmetic, body(): packed = jnp.take(joined_weight, stored, axis=2)  22.5 us
    reshape x1, local copies, waits for them, and re-layouts, body(): paired = weights_in.reshape(count, weights_in.shape[1], ff_local, 2)  18.4 us
    dot_general x1, matrix products, body(): jnp.einsum('ntf,nfd->td', active, down_weight, preferred_element_type=jnp...  14 us
  transfers between devices with their start and end apart: 1, of which 1 were waited for; matrix products, arithmetic and copies ran while one was open for 11% of the time, Pallas kernels for 0%

profile of v1, /device:TPU:0, one launch (start us, length us, event | category | flops | bytes accessed | tf_op | source)
XLA Modules:
  0.0 370.5 jit_solution(16177325848410322226)
XLA Ops:
  0.6 0.0 copy-start
  0.7 0.9 select_reduce_fusion.1
  1.6 0.6 select_reduce_fusion
  2.2 19.8 %copy.44 = bf16[2,180,5760]{1,0,2:T(2,128)(2,1)} copy(bf16[2,180,5760]{2,0,1:T(2,128)(2,1)} %param.6) | data formatting | bytes 8294400 | tf_op args[0]
  22.0 0.1 fusion.22
  22.2 25.1 %gather_fusion = bf16[5760,2,180]{2,1,0:T(2,128)(2,1)} fusion(bf16[2,180,5760]{1,0,2:T(2,128)(2,1)} %copy.44, s32[6144]{0:T(1024)S(1)} %pad_clamp_fusion), kind=kCustom, calls=%fused_computation | custom fusion | bytes 8317440 | tf_op jit(solution)/shard_map/jit(_take)/gather | solution.py:19
  47.2 22.3 %fusion.4 = bf16[2,180,5760]{1,0,2:T(2,128)(2,1)S(1)} fusion(bf16[5760,2,180]{2,1,0:T(2,128)(2,1)} %gather_fusion, pred[5760]{0:T(1024)(128)(4,1)S(1)} %compare_and_fusion), kind=kLoop, calls=%fused_computation.8 | loop fusion | flops 2073600 | bytes 8300160 | tf_op jit(solution)/shard_map/jit(_take)/select_n | solution.py:19
  69.5 0.0 copy-start.4
  69.6 76.8 %all_to_all.20 = bf16[2,180,5760]{1,0,2:T(2,128)(2,1)} all-to-all(bf16[2,180,5760]{1,0,2:T(2,128)(2,1)S(1)} %fusion.4), channel_id=1, replica_groups=mesh['row'=8,'col'=16] {'col'}, dimensions={2} | all-to-all | bytes 8294400 | tf_op jit(solution)/shard_map/all_to_all | solution.py:31
  146.4 0.0 copy-done.4
  146.4 3.0 stack.2
  149.4 7.5 %all-to-all-start.1 = ((bf16[128,8,2880]{2,1,0:T(8,128)(2,1)}), bf16[128,8,2880]{2,1,0:T(8,128)(2,1)}, u32[]{:S(2)}, u32[]{:S(2)}) async-start(bf16[128,8,2880]{2,1,0:T(8,128)(2,1)} %stack.2), calls=%async_computation.1 | async-start | bytes 12058624 | tf_op jit(solution)/shard_map/all_to_all | solution.py:24
  156.8 0.0 copy-done.3
  156.9 0.0 copy-done.5
  156.9 0.1 select_reduce_fusion.2
  157.0 7.3 %copy.63 = bf16[2,180,16,360]{1,2,3,0:T(8,128)(2,1)} copy(bf16[2,180,16,360]{1,0,3,2:T(2,128)(2,1)} %bitcast.39) | data formatting | bytes 8294400 | tf_op jit(solution)/shard_map/all_to_all | solution.py:31
  164.4 18.4 %reshape.84 = bf16[2,2880,180,2]{1,3,2,0:T(2,128)(2,1)} reshape(bf16[2,16,180,360]{2,1,3,0:T(8,128)(2,1)} %bitcast.40) | data formatting | bytes 8294400 | tf_op jit(solution)/shard_map/reshape | solution.py:33
  182.8 9.4 %fusion.25 = (bf16[2,2880,180,1]{1,3,2,0:T(2,128)(2,1)S(1)}, bf16[2,2880,180,1]{1,3,2,0:T(2,128)(2,1)S(1)}) fusion(bf16[2,2880,180,2]{1,3,2,0:T(2,128)(2,1)} %reshape.84), kind=kLoop, calls=%fused_computation.44 | loop fusion | bytes 8294400 | tf_op jit(solution)/shard_map/slice | solution.py:35
  192.2 0.2 copy.64
  192.4 0.0 copy-start.1
  192.4 3.0 copy.50
  195.4 0.2 copy.65
  195.6 0.0 copy-done.1
  195.6 0.0 copy-start.2
  195.7 1.3 copy-done.2
  197.0 3.0 copy.51
  199.9 29.0 %all-to-all-done.1 = bf16[128,8,2880]{2,1,0:T(8,128)(2,1)} async-done(((bf16[128,8,2880]{2,1,0:T(8,128)(2,1)}), bf16[128,8,2880]{2,1,0:T(8,128)(2,1)}, u32[]{:S(2)}, u32[]{:S(2)}) %all-to-all-start.1) | async-done | bytes 5898272 | tf_op jit(solution)/shard_map/all_to_all | solution.py:24
  228.9 7.0 %fusion = f32[2,180,1024]{2,1,0:T(8,128)} fusion(bf16[2,2880,180]{1,2,0:T(8,128)(2,1)} %bitcast.42, bf16[128,8,2880]{2,1,0:T(8,128)(2,1)} %all-to-all-done.1), kind=kOutput, calls=%fused_computation.3 | convolution fusion | flops 2123366400 | bytes 9446400 | tf_op jit(solution)/shard_map/td,ndf->ntf/dot_general | solution.py:36
  235.9 0.0 copy-done
  235.9 14.0 %convolution_bitcast_fusion = f32[1024,2880]{1,0:T(8,128)} fusion(bf16[2,180,2880]{2,0,1:T(2,128)(2,1)S(1)} %copy-done, f32[2,180,1024]{2,1,0:T(8,128)} %fusion, bf16[2,2880,180]{1,2,0:T(8,128)(2,1)} %bitcast.44, bf16[128,8,2880]{2,1,0:T(8,128)(2,1)} %all-to-all-done.1, f32[2,1024]{1,0:T(2,128)S(1)} %bitcast.45), kind=kOutput, calls=%fused_computation.2 | convolution fusion | flops 4250050560 | bytes 23324672 | tf_op jit(solution)/shard_map/ntf,nfd->td/dot_general | solution.py:43
  250.0 119.1 %all-reduce.2 = bf16[1024,2880]{1,0:T(8,128)(2,1)} all-reduce(f32[1024,2880]{1,0:T(8,128)} %convolution_bitcast_fusion), channel_id=2, replica_groups=mesh['row'=8,'col'=16] {'row','col'}, use_global_device_ids=true, to_apply=%region_4.5.clone | all-reduce | flops 2949120 | bytes 17694720
  369.1 1.4 dynamic-slice_convert_fusion
  (9 shorter events, 0.1 us)
Async XLA Ops:
  0.6 235.3 %copy-start = (bf16[2,180,2880]{2,0,1:T(2,128)(2,1)S(1)}, bf16[2,180,2880]{2,0,1:T(2,128)(2,1)}, u32[]{:S(2)}) copy-start(bf16[2,180,2880]{2,0,1:T(2,128)(2,1)} %param.8) | copy-start | bytes 6220804
  69.5 76.8 %copy-start.4 = (bf16[8,2880]{1,0:T(8,128)(2,1)S(1)}, bf16[8,2880]{1,0:T(8,128)(2,1)}, u32[]{:S(2)}) copy-start(bf16[8,2880]{1,0:T(8,128)(2,1)} %param.9) | copy-start | bytes 138244
  149.4 7.5 %copy-start.3 = (f32[1024,4]{0,1:T(4,128)S(1)}, f32[1024,4]{0,1:T(4,128)}, u32[]{:S(2)}) copy-start(f32[1024,4]{0,1:T(4,128)} %param.11) | copy-start | bytes 49156
  149.4 7.5 %copy-start.5 = (s32[1024,4]{0,1:T(4,128)S(1)}, s32[1024,4]{0,1:T(4,128)}, u32[]{:S(2)}) copy-start(s32[1024,4]{0,1:T(4,128)} %param.10) | copy-start | bytes 49156
  149.4 79.5 %all-to-all-start.1 = ((bf16[128,8,2880]{2,1,0:T(8,128)(2,1)}), bf16[128,8,2880]{2,1,0:T(8,128)(2,1)}, u32[]{:S(2)}, u32[]{:S(2)}) async-start(bf16[128,8,2880]{2,1,0:T(8,128)(2,1)} %stack.2), calls=%async_computation.1 | async-start | bytes 12058624 | tf_op jit(solution)/shard_map/all_to_all | solution.py:24
  192.4 3.2 copy-start.1
  195.6 1.3 copy-start.2
